TPU v7x, 32 devices: a whole 2x2x4 slice. The times are simulated.
32 devices in a mesh: leaf: 16 (over z, y, x), sep: 2 (over core).
Axes of the slice: x: 2, y: 2, z: 4, core: 2. Of those that a mesh axis runs over, the one named last changes fastest.
Arguments:
- leaf_rhs: bfloat16 [16, 256, 2048], P('leaf', None, 'sep'), may hold values from -6 to 6
- leaf_inv: bfloat16 [16, 2048, 2048], P('leaf', 'sep'), may hold values from -0.125 to 0.125
- leaf_couple: bfloat16 [16, 512, 2048], P('leaf', None, 'sep'), may hold values from -0.0625 to 0.0625
- sep_rhs: float32 [16, 256, 512], P('leaf', None, 'sep'), may hold values from -6 to 6
- sep_inv: float32 [16, 512, 512], P('leaf', 'sep'), may hold values from -0.25 to 0.25
- sep_couple: float32 [16, 512, 512], P('leaf', None, 'sep'), may hold values from -0.1875 to 0.1875
Outputs:
- leaf_solution: float32 [16, 256, 2048], P('leaf', None, 'sep')
- sep_solution: float32 [16, 256, 512], P('leaf', None, 'sep')
All inputs are finite; a program needn't handle non-finite values.
Results may differ from a plain program's by a relative error of at most 0.0042.
Values may be sent and summed in bfloat16 or wider, within the bound.
A program may use at most 128 MiB of HBM per device.

v0:
```python
import jax
import jax.numpy as jnp
from jax import lax
from jax.sharding import PartitionSpec as P


def partner(value, axis, apart):
    mask = 2**apart
    pairs = [(source, source ^ mask) for source in range(lax.axis_size(axis))]
    return lax.ppermute(value, axis, pairs)


def times_transposed(left, right):
    return lax.dot_general(
        left,
        right,
        (((1,), (1,)), ((), ())),
        precision=lax.Precision.HIGHEST,
        preferred_element_type=jnp.float32,
    )


def times_plain(left, right):
    return jnp.dot(left, right, precision=lax.Precision.HIGHEST, preferred_element_type=jnp.float32)


def device_level(place, depth):
    level = jnp.int32(1)
    running = jnp.bool_(True)
    for bit in range(depth + 1):
        running = running & (place >> bit & 1 == 1)
        level = level + running.astype(jnp.int32)
    return level


def local(leaf_rhs, leaf_inv, leaf_couple, sep_rhs, sep_inv, sep_couple):
    depth = lax.axis_size("leaf").bit_length() - 1
    place = lax.axis_index("leaf")
    level = device_level(place, depth)
    rhs_local = leaf_rhs[0]
    inv_rows = leaf_inv[0]
    couple_cols = leaf_couple[0]
    sep_local = sep_rhs[0]
    sep_rows = sep_inv[0]
    sep_cols = sep_couple[0]
    rows = rhs_local.shape[0]
    half_sep = sep_rows.shape[0]
    width = sep_rows.shape[1]
    leaf_forward = lax.dot_general(
        lax.all_gather(rhs_local, "sep", axis=1, tiled=True),
        inv_rows,
        (((1,), (1,)), ((), ())),
        preferred_element_type=jnp.float32,
    )
    leaf_state = leaf_forward.astype(jnp.bfloat16)
    outgoing = lax.dot_general(
        leaf_state, couple_cols, (((1,), (1,)), ((), ())), preferred_element_type=jnp.float32
    )
    carry_rhs, carry_inv, carry_cols = (sep_local, sep_rows, sep_cols)
    ancestry = []
    for bit in range(depth):
        other_rhs, other_inv, other_cols = partner((carry_rhs, carry_inv, carry_cols), "leaf", bit)
        is_upper = place >> bit & 1 == 1
        ancestry.append(
            (
                jnp.where(is_upper, other_rhs, carry_rhs),
                jnp.where(is_upper, other_inv, carry_inv),
                jnp.where(is_upper, other_cols, carry_cols),
            )
        )
        carry_rhs = jnp.where(is_upper, carry_rhs, other_rhs)
        carry_inv = jnp.where(is_upper, carry_inv, other_inv)
        carry_cols = jnp.where(is_upper, carry_cols, other_cols)
    ancestry.append((carry_rhs, carry_inv, carry_cols))
    states = []
    mine = outgoing
    for section in range(1, depth + 2):
        rhs_half, inv_part, cols_part = ancestry[section - 1]
        share = lax.psum_scatter(mine, "sep", scatter_dimension=1, tiled=True)
        total = share
        if section <= depth:
            total = share + partner(share, "leaf", section - 1)
        whole_work = lax.all_gather(rhs_half - total, "sep", axis=1, tiled=True)
        fresh = times_transposed(whole_work, inv_part)
        states.append(fresh)
        if section <= depth:
            mine = times_transposed(fresh, cols_part)
    sep_solution = jnp.zeros((rows, half_sep), jnp.float32)
    parent_full = jnp.zeros((rows, width), jnp.float32)
    for section in range(depth + 1, 0, -1):
        rhs_half, inv_part, cols_part = ancestry[section - 1]
        if section == depth + 1:
            work = states[section - 1]
        else:
            work = states[section - 1] - times_plain(parent_full, cols_part)
        partial_value = times_plain(work, inv_part)
        current = lax.psum_scatter(partial_value, "sep", scatter_dimension=1, tiled=True)
        sep_solution = jnp.where(level == section, current, sep_solution)
        parent_full = lax.all_gather(current, "sep", axis=1, tiled=True)
    pulled = jnp.dot(
        parent_full.astype(jnp.bfloat16), couple_cols, preferred_element_type=jnp.float32
    )
    residue = (leaf_state.astype(jnp.float32) - pulled).astype(jnp.bfloat16)
    spread = jnp.dot(residue, inv_rows, preferred_element_type=jnp.float32)
    leaf_solution = lax.psum_scatter(spread, "sep", scatter_dimension=1, tiled=True)
    return (leaf_solution[None], sep_solution[None])


def solution(mesh):
    return jax.shard_map(
        local,
        mesh=mesh,
        in_specs=(
            P("leaf", None, "sep"),
            P("leaf", "sep", None),
            P("leaf", None, "sep"),
            P("leaf", None, "sep"),
            P("leaf", "sep", None),
            P("leaf", None, "sep"),
        ),
        out_specs=(P("leaf", None, "sep"), P("leaf", None, "sep")),
        check_vma=False,
    )
```

profile of v0, /device:TPU:11, one launch (start us, length us, event | category | flops | bytes accessed | tf_op | source)
XLA Modules:
  0.0 327.8 jit_solution(13412599410338617865)
XLA Ops:
  8.0 12.5 %all-gather.3.cloned.1.call-done = bf16[1,256,2048]{2,1,0:T(8,128)(2,1)} async-done(((bf16[1,256,1024]{2,1,0:T(8,128)(2,1)}), bf16[1,256,2048]{2,1,0:T(8,128)(2,1)}) %all-gather.3.cloned.1.call-update) | async-done | bytes 1048592 | tf_op jit(solution)/shard_map/all_gather | solution.py:50
  26.8 8.9 %reduce-scatter.12.cloned.1.call-done = f32[256,256]{1,0:T(8,128)} async-done(((f32[256,512]{1,0:T(8,128)}), f32[256,256]{1,0:T(8,128)}) %reduce-scatter.12.cloned.1.call-update) | async-done | bytes 262160 | tf_op jit(solution)/shard_map/reduce_scatter | solution.py:79
  37.4 6.3 %collective-permute-done.1 = f32[256,256]{1,0:T(8,128)} collective-permute-done((f32[256,256]{1,0:T(8,128)}, f32[256,256]{1,0:T(8,128)}, u32[]{:S(2)}, u32[]{:S(2)}) %collective-permute-start.1) | collective-permute-done | bytes 262176 | tf_op jit(solution)/shard_map/ppermute | solution.py:10
  49.0 5.8 %collective-permute-done.2 = f32[256,512]{1,0:T(8,128)S(1)} collective-permute-done((f32[256,512]{1,0:T(8,128)S(1)}, f32[256,512]{1,0:T(8,128)S(1)}, u32[]{:S(2)}, u32[]{:S(2)}) %collective-permute-start.2) | collective-permute-done | bytes 524320 | tf_op jit(solution)/shard_map/ppermute | solution.py:10
  55.4 10.6 %collective-permute-done.4 = f32[512,256]{1,0:T(8,128)S(1)} collective-permute-done((f32[512,256]{1,0:T(8,128)S(1)}, f32[512,256]{1,0:T(8,128)S(1)}, u32[]{:S(2)}, u32[]{:S(2)}) %collective-permute-start.4) | collective-permute-done | bytes 524320 | tf_op jit(solution)/shard_map/ppermute | solution.py:10
  69.2 8.4 %reduce-scatter.14.cloned.1.call-done = f32[256,256]{1,0:T(8,128)} async-done(((f32[256,512]{1,0:T(8,128)}), f32[256,256]{1,0:T(8,128)}) %reduce-scatter.14.cloned.1.call-update) | async-done | bytes 262160 | tf_op jit(solution)/shard_map/reduce_scatter | solution.py:79
  79.2 6.7 %collective-permute-done.3 = f32[256,256]{1,0:T(8,128)} collective-permute-done((f32[256,256]{1,0:T(8,128)}, f32[256,256]{1,0:T(8,128)}, u32[]{:S(2)}, u32[]{:S(2)}) %collective-permute-start.3) | collective-permute-done | bytes 262176 | tf_op jit(solution)/shard_map/ppermute | solution.py:10
  85.9 5.5 %collective-permute-done.5 = f32[256,256]{1,0:T(8,128)S(1)} collective-permute-done((f32[256,256]{1,0:T(8,128)}, f32[256,256]{1,0:T(8,128)S(1)}, u32[]{:S(2)}, u32[]{:S(2)}) %collective-permute-start.5) | collective-permute-done | bytes 262176 | tf_op jit(solution)/shard_map/ppermute | solution.py:10
  93.3 5.1 %all_gather.35 = f32[256,512]{1,0:T(8,128)S(1)} all-gather(f32[256,256]{1,0:T(8,128)S(1)} %get-tuple-element.5), channel_id=1, replica_groups=mesh['leaf'=16,'sep'=2] {'sep'}, dimensions={1}, use_global_device_ids=true | all-gather | bytes 786432 | tf_op jit(solution)/shard_map/all_gather | solution.py:83
  106.9 8.3 %reduce-scatter.16.cloned.1.call-done = f32[256,256]{1,0:T(8,128)} async-done(((f32[256,512]{1,0:T(8,128)}), f32[256,256]{1,0:T(8,128)}) %reduce-scatter.16.cloned.1.call-update) | async-done | bytes 262160 | tf_op jit(solution)/shard_map/reduce_scatter | solution.py:79
  122.7 5.5 %collective-permute-done.9 = f32[256,256]{1,0:T(8,128)S(1)} collective-permute-done((f32[256,256]{1,0:T(8,128)}, f32[256,256]{1,0:T(8,128)S(1)}, u32[]{:S(2)}, u32[]{:S(2)}) %collective-permute-start.9) | collective-permute-done | bytes 262176 | tf_op jit(solution)/shard_map/ppermute | solution.py:10
  130.1 6.9 %all_gather.36 = f32[256,512]{1,0:T(8,128)S(1)} all-gather(f32[256,256]{1,0:T(8,128)S(1)} %get-tuple-element.3), channel_id=1, replica_groups=mesh['leaf'=16,'sep'=2] {'sep'}, dimensions={1}, use_global_device_ids=true | all-gather | bytes 786432 | tf_op jit(solution)/shard_map/all_gather | solution.py:83
  145.4 7.4 %reduce-scatter.18.cloned.1.call-done = f32[256,256]{1,0:T(8,128)} async-done(((f32[256,512]{1,0:T(8,128)}), f32[256,256]{1,0:T(8,128)}) %reduce-scatter.18.cloned.1.call-update) | async-done | bytes 262160 | tf_op jit(solution)/shard_map/reduce_scatter | solution.py:79
  155.2 40.9 %collective-permute-done.11 = f32[256,256]{1,0:T(8,128)} collective-permute-done((f32[256,256]{1,0:T(8,128)}, f32[256,256]{1,0:T(8,128)}, u32[]{:S(2)}, u32[]{:S(2)}) %collective-permute-start.11) | collective-permute-done | bytes 262176 | tf_op jit(solution)/shard_map/ppermute | solution.py:10
  196.2 5.6 %collective-permute-done.13 = f32[256,256]{1,0:T(8,128)S(1)} collective-permute-done((f32[256,256]{1,0:T(8,128)}, f32[256,256]{1,0:T(8,128)S(1)}, u32[]{:S(2)}, u32[]{:S(2)}) %collective-permute-start.13) | collective-permute-done | bytes 262176 | tf_op jit(solution)/shard_map/ppermute | solution.py:10
  205.9 7.0 %collective-permute-done.15 = f32[512,256]{1,0:T(8,128)S(1)} collective-permute-done((f32[512,256]{1,0:T(8,128)S(1)}, f32[512,256]{1,0:T(8,128)S(1)}, u32[]{:S(2)}, u32[]{:S(2)}) %collective-permute-start.15) | collective-permute-done | bytes 524320 | tf_op jit(solution)/shard_map/ppermute | solution.py:10
  215.3 9.7 %reduce-scatter.20.cloned.1.call-done = f32[256,256]{1,0:T(8,128)} async-done(((f32[256,512]{1,0:T(8,128)}), f32[256,256]{1,0:T(8,128)}) %reduce-scatter.20.cloned.1.call-update) | async-done | bytes 262160 | tf_op jit(solution)/shard_map/reduce_scatter | solution.py:79
  232.5 7.3 %reduce-scatter.22.cloned.1.call-done = f32[256,256]{1,0:T(8,128)} async-done(((f32[256,512]{1,0:T(8,128)}), f32[256,256]{1,0:T(8,128)}) %reduce-scatter.22.cloned.1.call-update) | async-done | bytes 262160 | tf_op jit(solution)/shard_map/reduce_scatter | solution.py:97
  245.6 10.2 %reduce-scatter.24.cloned.1.call-done = f32[256,256]{1,0:T(8,128)} async-done(((f32[256,512]{1,0:T(8,128)}), f32[256,256]{1,0:T(8,128)}) %reduce-scatter.24.cloned.1.call-update) | async-done | bytes 262160 | tf_op jit(solution)/shard_map/reduce_scatter | solution.py:97
  262.6 9.1 %reduce-scatter.26.cloned.1.call-done = f32[256,256]{1,0:T(8,128)} async-done(((f32[256,512]{1,0:T(8,128)}), f32[256,256]{1,0:T(8,128)}) %reduce-scatter.26.cloned.1.call-update) | async-done | bytes 262160 | tf_op jit(solution)/shard_map/reduce_scatter | solution.py:97
  277.2 10.4 %reduce-scatter.28.cloned.1.call-done = f32[256,256]{1,0:T(8,128)} async-done(((f32[256,512]{1,0:T(8,128)}), f32[256,256]{1,0:T(8,128)}) %reduce-scatter.28.cloned.1.call-update) | async-done | bytes 262160 | tf_op jit(solution)/shard_map/reduce_scatter | solution.py:97
  293.2 9.2 %reduce-scatter.30.cloned.1.call-done = f32[256,256]{1,0:T(8,128)} async-done(((f32[256,512]{1,0:T(8,128)}), f32[256,256]{1,0:T(8,128)}) %reduce-scatter.30.cloned.1.call-update) | async-done | bytes 262160 | tf_op jit(solution)/shard_map/reduce_scatter | solution.py:97
  304.7 5.3 %fusion = f32[256,2048]{1,0:T(8,128)} fusion(bf16[1,1024,2048]{2,1,0:T(8,128)(2,1)} %param.7, bf16[1,512,1024]{2,1,0:T(8,128)(2,1)S(1)} %copy-done, bf16[256,1024]{1,0:T(8,128)(2,1)} %copy-done.21, f32[256,512]{1,0:T(8,128)S(1)} %all_gather.43), kind=kOutput, calls=%fused_computation | convolution fusion | flops 1343094784 | bytes 8388608 | tf_op jit(solution)/shard_map/dot_general | solution.py:104
  311.0 10.0 %reduce-scatter.32.cloned.1.call-done = f32[256,1024]{1,0:T(8,128)} async-done(((f32[256,2048]{1,0:T(8,128)}), f32[256,1024]{1,0:T(8,128)}) %reduce-scatter.32.cloned.1.call-update) | async-done | bytes 1048592 | tf_op jit(solution)/shard_map/reduce_scatter | solution.py:105
  (133 shorter events, 90.7 us)
Async XLA Ops:
  7.9 27.7 %reduce-scatter.12.cloned.1.call-start = ((), (), s32[]{:S(2)}) async-start(), calls=%async_computation.11 | async-start | bytes 786432 | tf_op jit(solution)/shard_map/reduce_scatter | solution.py:79
  26.4 51.2 %reduce-scatter.14.cloned.1.call-start = ((), (), s32[]{:S(2)}) async-start(), calls=%async_computation.12 | async-start | bytes 786432 | tf_op jit(solution)/shard_map/reduce_scatter | solution.py:79
  35.9 18.9 %collective-permute-start.2 = (f32[256,512]{1,0:T(8,128)S(1)}, f32[256,512]{1,0:T(8,128)S(1)}, u32[]{:S(2)}, u32[]{:S(2)}) collective-permute-start(f32[256,512]{1,0:T(8,128)S(1)} %bitcast.63), channel_id=1, source_target_pairs={{0,2},{2,0},{4,6},{6,4},{8,10},{10,8},{12,14},{14,12},{16,18},{18,... | collective-permute-start | bytes 1572872 | tf_op jit(solution)/shard_map/ppermute | solution.py:10
  37.1 28.9 %collective-permute-start.4 = (f32[512,256]{1,0:T(8,128)S(1)}, f32[512,256]{1,0:T(8,128)S(1)}, u32[]{:S(2)}, u32[]{:S(2)}) collective-permute-start(f32[512,256]{1,0:T(8,128)S(1)} %bitcast.62), channel_id=1, source_target_pairs={{0,2},{2,0},{4,6},{6,4},{8,10},{10,8},{12,14},{14,12},{16,18},{18,... | collective-permute-start | bytes 1572872 | tf_op jit(solution)/shard_map/ppermute | solution.py:10
  67.5 47.7 %reduce-scatter.16.cloned.1.call-start = ((), (), s32[]{:S(2)}) async-start(), calls=%async_computation.13 | async-start | bytes 786432 | tf_op jit(solution)/shard_map/reduce_scatter | solution.py:79
  67.7 30.8 %collective-permute-start.6 = (f32[256,512]{1,0:T(8,128)S(1)}, f32[256,512]{1,0:T(8,128)}, u32[]{:S(2)}, u32[]{:S(2)}) collective-permute-start(f32[256,512]{1,0:T(8,128)S(1)} %broadcast_select_fusion.13), channel_id=1, source_target_pairs={{0,4},{2,6},{4,0},{6,2},{8,12},{10,14},{12,8},{14,10},{16,20},{18,... | collective-permute-start | bytes 1572872 | tf_op jit(solution)/shard_map/ppermute | solution.py:10
  68.9 17.0 %collective-permute-start.3 = (f32[256,256]{1,0:T(8,128)}, f32[256,256]{1,0:T(8,128)}, u32[]{:S(2)}, u32[]{:S(2)}) collective-permute-start(f32[256,256]{1,0:T(8,128)} %get-tuple-element.6), channel_id=1, source_target_pairs={{0,4},{2,6},{4,0},{6,2},{8,12},{10,14},{12,8},{14,10},{16,20},{18,... | collective-permute-start | bytes 786440 | tf_op jit(solution)/shard_map/ppermute | solution.py:10
  77.6 13.9 %collective-permute-start.5 = (f32[256,256]{1,0:T(8,128)}, f32[256,256]{1,0:T(8,128)S(1)}, u32[]{:S(2)}, u32[]{:S(2)}) collective-permute-start(f32[256,256]{1,0:T(8,128)} %reduce-scatter.14.cloned.1.call-done), channel_id=1, source_target_pairs={{0,4},{2,6},{4,0},{6,2},{8,12},{10,14},{12,8},{14,10},{16,20},{18,... | collective-permute-start | bytes 786440 | tf_op jit(solution)/shard_map/ppermute | solution.py:10
  78.8 23.8 %collective-permute-start.8 = (f32[512,256]{1,0:T(8,128)S(1)}, f32[512,256]{1,0:T(8,128)S(1)}, u32[]{:S(2)}, u32[]{:S(2)}) collective-permute-start(f32[512,256]{1,0:T(8,128)S(1)} %broadcast_select_fusion.11), channel_id=1, source_target_pairs={{0,4},{2,6},{4,0},{6,2},{8,12},{10,14},{12,8},{14,10},{16,20},{18,... | collective-permute-start | bytes 1572872 | tf_op jit(solution)/shard_map/ppermute | solution.py:10
  104.1 48.6 %reduce-scatter.18.cloned.1.call-start = ((), (), s32[]{:S(2)}) async-start(), calls=%async_computation.14 | async-start | bytes 786432 | tf_op jit(solution)/shard_map/reduce_scatter | solution.py:79
  105.3 31.6 %collective-permute-start.10 = (f32[256,512]{1,0:T(8,128)S(1)}, f32[256,512]{1,0:T(8,128)}, u32[]{:S(2)}, u32[]{:S(2)}) collective-permute-start(f32[256,512]{1,0:T(8,128)S(1)} %broadcast_select_fusion.9), channel_id=1, source_target_pairs={{0,8},{2,10},{4,12},{6,14},{8,0},{10,2},{12,4},{14,6},{16,24},{18,... | collective-permute-start | bytes 1572872 | tf_op jit(solution)/shard_map/ppermute | solution.py:10
  105.6 17.1 %collective-permute-start.7 = (f32[256,256]{1,0:T(8,128)}, f32[256,256]{1,0:T(8,128)}, u32[]{:S(2)}, u32[]{:S(2)}) collective-permute-start(f32[256,256]{1,0:T(8,128)} %get-tuple-element.4), channel_id=1, source_target_pairs={{0,8},{2,10},{4,12},{6,14},{8,0},{10,2},{12,4},{14,6},{16,24},{18,... | collective-permute-start | bytes 786440 | tf_op jit(solution)/shard_map/ppermute | solution.py:10
  116.5 22.9 %collective-permute-start.12 = (f32[512,256]{1,0:T(8,128)S(1)}, f32[512,256]{1,0:T(8,128)S(1)}, u32[]{:S(2)}, u32[]{:S(2)}) collective-permute-start(f32[512,256]{1,0:T(8,128)S(1)} %broadcast_select_fusion.7), channel_id=1, source_target_pairs={{0,8},{2,10},{4,12},{6,14},{8,0},{10,2},{12,4},{14,6},{16,24},{18,... | collective-permute-start | bytes 1572872 | tf_op jit(solution)/shard_map/ppermute | solution.py:10
  141.7 83.2 %reduce-scatter.20.cloned.1.call-start = ((), (), s32[]{:S(2)}) async-start(), calls=%async_computation.15 | async-start | bytes 786432 | tf_op jit(solution)/shard_map/reduce_scatter | solution.py:79
  142.9 62.4 %collective-permute-start.14 = (f32[256,512]{1,0:T(8,128)S(1)}, f32[256,512]{1,0:T(8,128)}, u32[]{:S(2)}, u32[]{:S(2)}) collective-permute-start(f32[256,512]{1,0:T(8,128)S(1)} %broadcast_select_fusion.5), channel_id=1, source_target_pairs={{0,16},{2,18},{4,20},{6,22},{8,24},{10,26},{12,28},{14,30},{16,0},... | collective-permute-start | bytes 1572872 | tf_op jit(solution)/shard_map/ppermute | solution.py:10
  145.1 51.1 %collective-permute-start.11 = (f32[256,256]{1,0:T(8,128)}, f32[256,256]{1,0:T(8,128)}, u32[]{:S(2)}, u32[]{:S(2)}) collective-permute-start(f32[256,256]{1,0:T(8,128)} %get-tuple-element.2), channel_id=1, source_target_pairs={{0,16},{2,18},{4,20},{6,22},{8,24},{10,26},{12,28},{14,30},{16,0},... | collective-permute-start | bytes 786440 | tf_op jit(solution)/shard_map/ppermute | solution.py:10
  152.7 49.1 %collective-permute-start.13 = (f32[256,256]{1,0:T(8,128)}, f32[256,256]{1,0:T(8,128)S(1)}, u32[]{:S(2)}, u32[]{:S(2)}) collective-permute-start(f32[256,256]{1,0:T(8,128)} %reduce-scatter.18.cloned.1.call-done), channel_id=1, source_target_pairs={{0,16},{2,18},{4,20},{6,22},{8,24},{10,26},{12,28},{14,30},{16,0},... | collective-permute-start | bytes 786440 | tf_op jit(solution)/shard_map/ppermute | solution.py:10
  154.9 58.0 %collective-permute-start.15 = (f32[512,256]{1,0:T(8,128)S(1)}, f32[512,256]{1,0:T(8,128)S(1)}, u32[]{:S(2)}, u32[]{:S(2)}) collective-permute-start(f32[512,256]{1,0:T(8,128)S(1)} %broadcast_select_fusion.3), channel_id=1, source_target_pairs={{0,16},{2,18},{4,20},{6,22},{8,24},{10,26},{12,28},{14,30},{16,0},... | collective-permute-start | bytes 1572872 | tf_op jit(solution)/shard_map/ppermute | solution.py:10
  215.2 24.5 %reduce-scatter.22.cloned.1.call-start = ((), (), s32[]{:S(2)}) async-start(), calls=%async_computation.16 | async-start | bytes 786432 | tf_op jit(solution)/shard_map/reduce_scatter | solution.py:97
  232.4 23.4 %reduce-scatter.24.cloned.1.call-start = ((), (), s32[]{:S(2)}) async-start(), calls=%async_computation.17 | async-start | bytes 786432 | tf_op jit(solution)/shard_map/reduce_scatter | solution.py:97
  245.5 26.2 %reduce-scatter.26.cloned.1.call-start = ((), (), s32[]{:S(2)}) async-start(), calls=%async_computation.18 | async-start | bytes 786432 | tf_op jit(solution)/shard_map/reduce_scatter | solution.py:97
  262.5 25.1 %reduce-scatter.28.cloned.1.call-start = ((), (), s32[]{:S(2)}) async-start(), calls=%async_computation.19 | async-start | bytes 786432 | tf_op jit(solution)/shard_map/reduce_scatter | solution.py:97
  277.1 25.2 %reduce-scatter.30.cloned.1.call-start = ((), (), s32[]{:S(2)}) async-start(), calls=%async_computation.20 | async-start | bytes 786432 | tf_op jit(solution)/shard_map/reduce_scatter | solution.py:97
  293.1 27.8 %reduce-scatter.32.cloned.1.call-start = ((), (), s32[]{:S(2)}) async-start(), calls=%async_computation.21 | async-start | bytes 3145728 | tf_op jit(solution)/shard_map/reduce_scatter | solution.py:105
  (27 other events, 407.7 us)
Sparse Core Ops, SparseCore 0:
  9.5 10.8 all-gather.2
  26.5 9.0 reduce-scatter.11
  67.6 9.8 reduce-scatter.13
  104.2 10.8 reduce-scatter.15
  141.8 10.8 reduce-scatter.17
  215.3 9.5 reduce-scatter.19
  232.5 7.1 reduce-scatter.21
  245.6 10.0 reduce-scatter.23
  262.6 9.0 reduce-scatter.25
  277.3 10.2 reduce-scatter.27
  293.3 9.0 reduce-scatter.29
  310.2 10.7 reduce-scatter.31
where the time goes:
time: 329 us; the launch traced here: 328 us
  waiting for transfers between devices  215 us (65%)
  matrix products  37.5 us (11%)
  blocking collectives  32.1 us (10%)
  between operations  14.6 us (4%)
  starting transfers between devices  13.6 us (4%)
  other arithmetic  12.2 us (4%)
    ppermute x16, waiting for transfers between devices, partner(): return lax.ppermute(value, axis, pairs)  103 us
    reduce_scatter x5, waiting for transfers between devices, local(): lax.psum_scatter(partial_value, 'sep', scatter_dimension=1, tiled=True)  46.2 us
    reduce_scatter x5, waiting for transfers between devices, local(): share = lax.psum_scatter(mine, 'sep', scatter_dimension=1, tiled=True)  42.6 us
    all_gather x5, blocking collectives, local(): whole_work = lax.all_gather(rhs_half - total, 'sep', axis=1, tiled=True)  20 us
    dot_general x9, matrix products, times_plain(): jnp.dot(left, right, precision=lax.Precision.HIGHEST, preferred_element_t...  16.1 us
    ppermute x16, starting transfers between devices, partner(): return lax.ppermute(value, axis, pairs)  13.1 us
    all_gather x1, waiting for transfers between devices, local(): lax.all_gather(rhs_local, 'sep', axis=1, tiled=True)  12.5 us
    all_gather x5, blocking collectives, local(): parent_full = lax.all_gather(current, 'sep', axis=1, tiled=True)  12.1 us
  transfers between devices with their start and end apart: 28, of which 24 were waited for; matrix products, arithmetic and copies ran while one was open for 4% of the time, Pallas kernels for 0%

commit v1 on v0

v1 whole, which is shorter than its diff:
```python
import functools

import jax
import jax.numpy as jnp
from jax import lax
from jax.experimental import pallas as pl
from jax.experimental.pallas import tpu as pltpu
from jax.sharding import PartitionSpec as P

F32 = jnp.float32
BF16 = jnp.bfloat16


def dot_nt(a, b):
    return lax.dot_general(a, b, (((1,), (1,)), ((), ())), preferred_element_type=F32)


def dot_nn(a, b):
    return lax.dot_general(a, b, (((1,), (0,)), ((), ())), preferred_element_type=F32)


def dot_tn(a, b):
    return lax.dot_general(a, b, (((0,), (0,)), ((), ())), preferred_element_type=F32)


def halves(value):
    high = value.astype(BF16)
    return high, (value - high.astype(F32)).astype(BF16)


def three_pass(a, b, dot):
    ah, al = halves(a)
    bh, bl = halves(b)
    return dot(ah, bh) + (dot(ah, bl) + dot(al, bh))


def two_pass(a, b, dot):
    rows = a.shape[0]
    both = dot(jnp.concatenate(halves(a), axis=0), b)
    return both[:rows] + both[rows:]


def kernel(
    leaves,
    rhs_ref, inv_hbm, couple_hbm, srhs_ref, sinv_ref, scpl_ref,
    leaf_out, sep_out,
    inv, couple, other_rhs, state, other_inv, other_cpl, fac, top,
    r1, rb, rt, part_send, part_own, part_recv, xs, xr, o1, yr,
    zs, zr, sols, dn, s2, s1, gath, fin_s, fin_r, sep_acc,
    load_sem, send_sem, recv_sem, rsend, rrecv, osend, orecv,
):
    p = lax.axis_index("leaf")
    c = lax.axis_index("sep")
    oc = 1 - c
    b0 = p % 2
    b1 = (p // 2) % 2
    q = p // 4
    planes = leaves // 4
    below_top = planes // 2 - 1
    xp = p + 1 - 2 * b0
    yp = p + 2 - 4 * b1
    rows = rhs_ref.shape[0]
    part = rhs_ref.shape[1]
    width = sinv_ref.shape[1]
    half = width // 2
    quarter = rows // 4
    eighth = rows // 8

    loads = [
        pltpu.make_async_copy(couple_hbm.at[0], couple, load_sem.at[0]),
        pltpu.make_async_copy(inv_hbm.at[0], inv, load_sem.at[1]),
    ]
    for copy in loads:
        copy.start()

    me = p * 2 + c
    count = 2 * leaves
    barrier = pltpu.get_barrier_semaphore()

    @pl.loop(1, count)
    def _(step):
        to = (me + step) % count
        pl.semaphore_signal(barrier, inc=1, device_id=(to // 2, to % 2), device_id_type=pl.DeviceIdType.MESH)

    pl.semaphore_wait(barrier, count - 1)

    pending = []

    def remote(src, dst, ssem, rsem, to):
        return pltpu.make_async_remote_copy(
            src_ref=src, dst_ref=dst, send_sem=ssem, recv_sem=rsem,
            device_id=to, device_id_type=pl.DeviceIdType.MESH,
        )

    def when(cond, action):
        if cond is None:
            action()
        else:
            @pl.when(cond)
            def _():
                action()

    def push(src, dst, ssem, rsem, to, cond=None):
        copy = remote(src, dst, ssem, rsem, to)
        when(cond, lambda: copy.start())
        pending.append((cond, copy))

    def arrive(dst, rsem, cond=None):
        copy = remote(dst, dst, send_sem.at[0], rsem, (p, oc))
        when(cond, lambda: copy.wait_recv())

    def send(src, dst, slot, to, cond=None):
        push(src, dst, send_sem.at[slot], recv_sem.at[slot], to, cond)

    def got(dst, slot, cond=None):
        arrive(dst, recv_sem.at[slot], cond)

    mate = (p, oc)
    send(sinv_ref, other_inv, 1, mate)
    send(scpl_ref.at[pl.ds(pl.multiple_of(oc * half, half), half)], other_cpl, 2, mate)
    send(rhs_ref, other_rhs, 0, mate)

    is_even = b0 == 0
    is_top = p == leaves - 1
    for t in range(4):
        tc, tb0 = t // 2, t % 2
        to = (p - b0 + tb0, tc)
        mine = (c == tc) & (b0 == tb0)
        push(
            srhs_ref.at[pl.ds(t * quarter, quarter)], r1.at[c], rsend.at[t], rrecv.at[c],
            to, is_even & jnp.logical_not(mine),
        )

        @pl.when(is_even & mine)
        def _():
            r1[c] = srhs_ref[pl.ds(t * quarter, quarter), :]

    is_odd = (b0 == 1) & jnp.logical_not(is_top)
    for t in range(8):
        tc, tb0, tb1 = t // 4, (t // 2) % 2, t % 2
        to = (4 * q + 2 * tb1 + tb0, tc)
        mine = (c == tc) & (b0 == tb0) & (b1 == tb1)
        block = srhs_ref.at[pl.ds(t * eighth, eighth)]
        push(block, rb.at[b1, c], rsend.at[4 + t], rrecv.at[2 + 2 * b1 + c], to, is_odd & jnp.logical_not(mine))

        @pl.when(is_odd & mine)
        def _():
            rb[b1, c] = srhs_ref[pl.ds(t * eighth, eighth), :]

        to = (4 * below_top + 2 * tb1 + tb0, tc)
        push(block, rt.at[c], rsend.at[12 + t], rrecv.at[6 + c], to, is_top)

    own = b0 * (1 + b1)
    got(other_inv, 1)
    got(other_cpl, 2)
    at = pl.ds(pl.multiple_of(c * half, half), half)
    ours = scpl_ref[at, :]
    m_rows = three_pass(ours, sinv_ref[...], dot_nn) + three_pass(other_cpl[...], other_inv[...], dot_nn)
    n_rows = three_pass(sinv_ref[:, at], sinv_ref[...], dot_tn) + three_pass(other_inv[:, at], other_inv[...], dot_tn)
    fac[0, own, c] = jnp.where(is_top, n_rows, m_rows).astype(BF16)
    fac[1, own, c] = n_rows.astype(BF16)
    theirs = (1 - b0) * (1 + b1)
    carried = 1 + b1
    across = 2 - b1

    def factor_x(kind):
        base = 3 + 5 * kind
        ref = fac.at[kind, own, c]
        send(ref, ref, base + 1, (xp, c))
        send(ref, ref, base, mate)

    def factor_y(kind):
        base = 3 + 5 * kind
        ref = fac.at[kind, theirs, c]
        got(ref, base + 1)
        ref2 = fac.at[kind, carried, c]
        send(ref2, ref2, base + 3, (yp, c))
        send(ref, ref, base + 2, mate)

    def factor_end(kind):
        base = 3 + 5 * kind
        ref = fac.at[kind, across, c]
        got(ref, base + 3)
        send(ref, ref, base + 4, mate)

    def factor_wait(kind, which):
        base = 3 + 5 * kind
        idx, slot = ((own, base), (theirs, base + 2), (across, base + 4))[which]
        got(fac.at[kind, idx, oc], slot)

    def factor(kind, idx):
        return fac[kind, idx].reshape(width, width)

    factor_x(0)

    got(other_rhs, 0)
    loads[1].wait()
    mine_cols = pl.ds(pl.multiple_of(c * part, part), part)
    other_cols = pl.ds(pl.multiple_of(oc * part, part), part)
    piece = part // 4
    for j in range(4):
        at_j = pl.ds(j * piece, piece)
        value = dot_nt(rhs_ref[...], inv[at_j, mine_cols]) + dot_nt(other_rhs[...], inv[at_j, other_cols])
        state[:, at_j] = value.astype(BF16)
    loads[0].wait()
    mid = rows // 2
    part_send[...] = dot_nt(
        state[pl.ds(pl.multiple_of(oc * mid, mid), mid), :], couple[...]
    ).reshape(2, quarter, width)
    send(part_send, part_recv, 13, mate)
    part_own[...] = dot_nt(
        state[pl.ds(pl.multiple_of(c * mid, mid), mid), :], couple[...]
    ).reshape(2, quarter, width)
    got(part_recv, 13)
    xs[...] = part_own[1 - b0] + part_recv[1 - b0]
    send(xs, xr, 14, (xp, c))
    factor_x(1)
    factor_y(0)
    factor_wait(0, 0)
    factor_wait(0, 1)

    for h in range(2):
        arrive(r1.at[h], rrecv.at[h], jnp.logical_not(is_even & (c == h)))
    got(xr, 14)
    taken = part_own[b0] + part_recv[b0] + xr[...]
    w1 = jnp.concatenate([r1[0], r1[1]], axis=1) - taken
    o1[...] = two_pass(w1, factor(0, 0), dot_nt).reshape(2, eighth, width)
    send(o1.at[1 - b1], yr, 15, (yp, c))
    factor_end(0)
    factor_wait(0, 2)
    last = q == planes - 1
    joint = q == below_top
    send(fac.at[0, 2, c], top.at[c], 16, (4 * below_top + p % 4, c), last)

    for h in range(2):
        arrive(rb.at[0, h], rrecv.at[2 + h], jnp.logical_not((b0 == 1) & (b1 == 0) & (c == h)))
    got(yr, 15)
    w2 = jnp.concatenate([rb[0, 0], rb[0, 1]], axis=1) - (o1[b1] + yr[...])
    out2 = two_pass(w2, factor(0, 1), dot_nt)
    even_plane = q % 2 == 0
    odd_plane = jnp.logical_not(even_plane)
    zs[0] = out2
    place = p % 4
    send(zs.at[0], zr.at[1], 19, (4 * (q - 1) + place, c), odd_plane)

    reach = 1
    for bit in range(leaves.bit_length()):
        reach = jnp.where((q + 1) % (2 ** (bit + 1)) == 0, 2 ** (bit + 1), reach)
    upper = (q // (2 * reach)) % 2 == 1
    parent = jnp.where(upper, q - reach, q + reach)
    has_node = jnp.logical_not(last)
    low_child = q - reach // 2
    high_child = q + reach // 2
    inner = odd_plane & has_node

    factor_y(1)
    got(top.at[c], 16, joint)
    send(top.at[c], top.at[c], 17, mate, joint)

    for h in range(2):
        arrive(rb.at[1, h], rrecv.at[4 + h], has_node & jnp.logical_not((b0 == 1) & (b1 == 1) & (c == h)))
    got(zr.at[0], 18, inner)
    got(zr.at[1], 19, has_node)
    w3_at = s2.at[0]

    @pl.when(has_node)
    def _():
        first = jnp.where(even_plane, zs[0], zr[0])
        w3 = jnp.concatenate([rb[1, 0], rb[1, 1]], axis=1) - (first + zr[1])
        w3_at[...] = w3
        zs[1] = two_pass(w3, factor(0, 2), dot_nt)

    climbs = has_node & jnp.logical_not(joint)
    up_slot = 18 + jnp.where(upper, 1, 0)
    push(
        zs.at[1], zr.at[jnp.where(upper, 1, 0)], send_sem.at[20], recv_sem.at[up_slot],
        (4 * parent + place, c), climbs,
    )

    factor_end(1)
    for h in range(2):
        arrive(rt.at[h], rrecv.at[6 + h], joint)
    got(top.at[oc], 17, joint)

    @pl.when(joint)
    def _():
        wt = jnp.concatenate([rt[0], rt[1]], axis=1) - zs[1]
        sols[0] = two_pass(wt, top[...].reshape(width, width), dot_nn)
    for which in range(3):
        factor_wait(1, which)

    w3n = two_pass(w3_at[...] if False else jnp.where(has_node, w3_at[...], 0.0), factor(1, 2), dot_nn)
    got(dn.at[0], 21, climbs)

    @pl.when(has_node)
    def _():
        above = jnp.where(joint, sols[0], dn[0])
        sols[1] = w3n - two_pass(above, factor(0, 2), dot_nn)

    push(sols.at[1], dn.at[0], send_sem.at[22], recv_sem.at[21], (4 * low_child + place, c), inner)
    push(sols.at[1], dn.at[0], send_sem.at[23], recv_sem.at[21], (4 * high_child + place, c), inner)
    push(sols.at[1], dn.at[1], send_sem.at[24], recv_sem.at[22], (4 * (q + 1) + place, c), even_plane)
    w2n = two_pass(w2, factor(1, 1), dot_nn)
    w1n = two_pass(w1, factor(1, 0), dot_nn)
    got(dn.at[1], 22, odd_plane)
    above2 = jnp.where(even_plane, sols[1], dn[1])
    s1[b1] = w2n - two_pass(above2, factor(0, 1), dot_nn)
    send(s1.at[b1], s1.at[b1], 25, (yp, c))
    got(s1.at[1 - b1], 25)
    sol1 = w1n - two_pass(s1[...].reshape(quarter, width), factor(0, 0), dot_nn)
    s2[...] = sol1.reshape(2, eighth, width)
    slot = c * 2 + b0
    gath[slot] = sol1.astype(BF16)
    for t in range(1, 4):
        to_c = (c + t // 2) % 2
        to_b = (b0 + t % 2) % 2
        push(
            gath.at[slot], gath.at[slot], osend.at[t], orecv.at[t], (p - b0 + to_b, to_c),
        )

    block8 = c * 4 + b0 * 2 + b1
    for h in range(2):
        cols = pl.ds(h * half, half)
        for part_at in range(2):
            block = 2 * slot + part_at
            to = (p - b0, h)
            mine = is_even & (c == h)
            push(
                s2.at[part_at, :, cols], sep_acc.at[block], osend.at[4 + 2 * h + part_at],
                orecv.at[4 + block], to, jnp.logical_not(mine),
            )

            @pl.when(mine)
            def _():
                sep_acc[block] = s2[part_at, :, cols]

        here = (b0 == 1) & (b1 == 0) & (c == h)
        push(s1.at[b1, :, cols], sep_acc.at[block8], osend.at[8 + h], orecv.at[4 + block8], (4 * q + 1, h), jnp.logical_not(here))

        @pl.when(here)
        def _():
            sep_acc[block8] = s1[b1, :, cols]

        here = (b0 == 1) & (b1 == 1) & (c == h)
        push(sols.at[1, :, cols], sep_acc.at[block8], osend.at[10 + h], orecv.at[4 + block8], (4 * q + 3, h), has_node & jnp.logical_not(here))

        @pl.when(here & has_node)
        def _():
            sep_acc[block8] = sols[1, :, cols]

        push(sols.at[0, :, cols], sep_acc.at[block8], osend.at[12 + h], orecv.at[4 + block8], (leaves - 1, h), joint)

    for t in range(1, 4):
        from_c = (c + t // 2) % 2
        from_b = (b0 + t % 2) % 2
        arrive(gath.at[from_c * 2 + from_b], orecv.at[t])

    whole = gath[...].reshape(rows, width)
    residue = (state[...].astype(F32) - dot_nn(whole, couple[...])).astype(BF16)
    for j in range(4):
        cols = pl.ds(pl.multiple_of(oc * part + j * piece, piece), piece)
        fin_s[j] = dot_nn(residue, inv[:, cols])
        send(fin_s.at[j], fin_r.at[j], 26 + j, mate)
    for j in range(4):
        cols = pl.ds(pl.multiple_of(c * part + j * piece, piece), piece)
        value = dot_nn(residue, inv[:, cols])
        got(fin_r.at[j], 26 + j)
        leaf_out[:, pl.ds(j * piece, piece)] = value + fin_r[j]

    for block in range(8):
        bc, bb0, bb1 = block // 4, (block // 2) % 2, block % 2
        self_even = is_even & (c == bc) & (bb0 == 0)
        self_odd = (b0 == 1) & jnp.logical_not(is_top) & (c == bc) & (bb0 == 1) & (b1 == bb1)
        arrive(sep_acc.at[block], orecv.at[4 + block], jnp.logical_not(self_even | self_odd))
    sep_out[...] = sep_acc[...].reshape(rows, half)

    for cond, copy in pending:
        when(cond, lambda copy=copy: copy.wait_send())


def local(leaves, leaf_rhs, leaf_inv, leaf_couple, sep_rhs, sep_inv, sep_couple):
    _, rows, part = leaf_rhs.shape
    full = leaf_inv.shape[2]
    width = sep_inv.shape[2]
    half = width // 2
    quarter, eighth = rows // 4, rows // 8
    vmem = pl.BlockSpec(memory_space=pltpu.VMEM)
    anywhere = pl.BlockSpec(memory_space=pl.ANY)
    V = pltpu.VMEM
    dma = pltpu.SemaphoreType.DMA
    leaf_solution, sep_solution = pl.pallas_call(
        functools.partial(kernel, leaves),
        out_shape=(
            jax.ShapeDtypeStruct((rows, part), F32),
            jax.ShapeDtypeStruct((rows, half), F32),
        ),
        in_specs=[vmem, anywhere, anywhere, vmem, vmem, vmem],
        out_specs=(vmem, vmem),
        scratch_shapes=[
            V((part, full), BF16), V((width, part), BF16), V((rows, part), BF16), V((rows, part), BF16),
            V((half, width), F32), V((half, half), F32), V((2, 3, 2, half, width), BF16), V((2, half, width), BF16),
            V((2, quarter, half), F32), V((2, 2, eighth, half), F32), V((2, eighth, half), F32),
            V((2, quarter, width), F32), V((2, quarter, width), F32), V((2, quarter, width), F32),
            V((quarter, width), F32), V((quarter, width), F32), V((2, eighth, width), F32), V((eighth, width), F32),
            V((2, eighth, width), F32), V((2, eighth, width), F32), V((2, eighth, width), F32), V((2, eighth, width), F32),
            V((2, eighth, width), F32), V((2, eighth, width), F32), V((4, quarter, width), BF16),
            V((4, rows, part // 4), F32), V((4, rows, part // 4), F32), V((8, eighth, half), F32),
            dma((2,)), dma((30,)), dma((30,)), dma((20,)), dma((8,)), dma((14,)), dma((12,)),
        ],
        compiler_params=pltpu.CompilerParams(
            collective_id=0, has_side_effects=True, vmem_limit_bytes=60 * 1024 * 1024
        ),
    )(leaf_rhs[0], leaf_inv, leaf_couple, sep_rhs[0], sep_inv[0], sep_couple[0])
    return leaf_solution[None], sep_solution[None]


def solution(mesh):
    return jax.shard_map(
        functools.partial(local, mesh.shape["leaf"]),
        mesh=mesh,
        in_specs=(
            P("leaf", None, "sep"),
            P("leaf", "sep", None),
            P("leaf", None, "sep"),
            P("leaf", None, "sep"),
            P("leaf", "sep", None),
            P("leaf", None, "sep"),
        ),
        out_specs=(P("leaf", None, "sep"), P("leaf", None, "sep")),
        check_vma=False,
    )
```

time: 329 us -> 64.8 us (0.20)
  waiting for transfers between devices: 215 us -> 0 us
  Pallas kernels: 0 us -> 59 us
  matrix products: 37.5 us -> 0 us
  blocking collectives: 32.1 us -> 0 us
  between operations: 14.6 us -> 0.64 us
  starting transfers between devices: 13.6 us -> 0 us
  other arithmetic: 12.2 us -> 0 us
    ppermute x16 -> x0, waiting for transfers between devices: 103 us -> none  [partner(): return lax.ppermute(value, axis, pairs)]
    reduce_scatter x11 -> x0, waiting for transfers between devices: 98.8 us -> none  [the longest x5 46.2 us: local(): lax.psum_scatter(partial_value, 'sep', scatter_dimension=1, tiled=True)]
    pallas_call x0 -> x1, Pallas kernels: none -> 59 us  [local(): pl.pallas_call(functools.partial(kernel, leaves), out_shape=(jax.ShapeDty...]
    dot_general x21 -> x0, matrix products: 37.5 us -> none  [the longest x9 16.1 us: times_plain(): jnp.dot(left, right, precision=lax.Precision.HIGHEST, preferred_element_t...]
    all_gather x10 -> x0, blocking collectives: 32.1 us -> none  [the longest x5 20 us: local(): whole_work = lax.all_gather(rhs_half - total, 'sep', axis=1, tiled=True)]
    ppermute x16 -> x0, starting transfers between devices: 13.1 us -> none  [partner(): return lax.ppermute(value, axis, pairs)]
    all_gather x1 -> x0, waiting for transfers between devices: 12.5 us -> none  [local(): lax.all_gather(rhs_local, 'sep', axis=1, tiled=True)]
    select_n x9 -> x0, other arithmetic: 9.23 us -> none  [the longest x3 5.63 us: local(): carry_rhs = jnp.where(is_upper, carry_rhs, other_rhs)]
  transfers between devices with their start and end apart: 28 -> 0, of which waited for: 24 -> 0; matrix products, arithmetic and copies ran while one was open for 4% -> 0% of each run, Pallas kernels for 0% -> 0%
where the time goes in v1:
time: 64.8 us; the launch traced here: 63.6 us
  Pallas kernels  59 us (91%)
  local copies, waits for them, and re-layouts  3.98 us (6%)
    pallas_call x1, Pallas kernels, local(): pl.pallas_call(functools.partial(kernel, leaves), out_shape=(jax.ShapeDty...  59 us
    unnamed x2, local copies, waits for them, and re-layouts  3.98 us

profile of v1, /device:TPU:11, one launch (start us, length us, event | category | flops | bytes accessed | tf_op | source)
XLA Modules:
  0.0 63.6 jit_solution(8752263326658550885)
XLA Ops:
  0.6 59.0 %shard_map.77 = (f32[256,1024]{1,0:T(8,128)}, f32[256,256]{1,0:T(8,128)}) custom-call(bf16[256,1024]{1,0:T(8,128)(2,1)} %bitcast.7, bf16[1,1024,2048]{2,1,0:T(8,128)(2,1)} %inv_hbm.1, bf16[1,512,1024]{2,1,0:T(8,128)(2,1)} %couple_hbm.1, f32[256,256]{1,0:T(8,128)} %bitcast.10, f32[256,512]{1,0:T(8,128)} %bitcast.8, f32[512,256]{1,0:T(8,128)} %bitcast.9), custom_call_target="tpu_custom_call" | custom-call | tf_op jit(solution)/shard_map/pallas_call | solution.py:391
  59.6 2.3 %copy.10 = f32[1,256,1024]{2,1,0:T(8,128)} copy(f32[1,256,1024]{2,1,0:T(8,128)} %bitcast.6) | data formatting | bytes 2097152
  61.9 1.7 %copy.11 = f32[1,256,256]{2,1,0:T(8,128)} copy(f32[1,256,256]{2,1,0:T(8,128)} %bitcast.11) | data formatting | bytes 524288

commit v2 on v1

--- a/solution.py
+++ b/solution.py
@@ -46,8 +46,8 @@
     leaf_out, sep_out,
     inv, couple, other_rhs, state, other_inv, other_cpl, fac, top,
     r1, rb, rt, part_send, part_own, part_recv, xs, xr, o1, yr,
-    zs, zr, sols, dn, s2, s1, gath, fin_s, fin_r, sep_acc,
-    load_sem, send_sem, recv_sem, rsend, rrecv, osend, orecv,
+    ys, zs, zb, zr, sols, sb, dn, s2, s1, sh, gath, fin_s, fin_r, sep_acc,
+    load_sem, send_sem, recv_sem, fsend, frecv, rsend, rrecv, osend, orecv, gsend, grecv,
 ):
     p = lax.axis_index("leaf")
     c = lax.axis_index("sep")
@@ -160,33 +160,41 @@
     fac[0, own, c] = jnp.where(is_top, n_rows, m_rows).astype(BF16)
     fac[1, own, c] = n_rows.astype(BF16)
     theirs = (1 - b0) * (1 + b1)
-    carried = 1 + b1
     across = 2 - b1
 
+    chunk = half // 4
+
+    def share(kind, idx, path, i, to, cond=None):
+        ref = fac.at[kind, idx, c, pl.ds(i * chunk, chunk)]
+        push(ref, ref, fsend.at[kind, path, i], frecv.at[kind, 1 if path == 4 else path, i], to, cond)
+
+    def shared(kind, idx, core, path, i):
+        arrive(fac.at[kind, idx, core, pl.ds(i * chunk, chunk)], frecv.at[kind, path, i])
+
     def factor_x(kind):
-        base = 3 + 5 * kind
+        for i in range(4):
+            share(kind, own, 0, i, (xp, c))
+            share(kind, own, 1, i, (yp, c), b0 == 1)
         ref = fac.at[kind, own, c]
-        send(ref, ref, base + 1, (xp, c))
-        send(ref, ref, base, mate)
+        send(ref, ref, 3 + kind, mate)
 
     def factor_y(kind):
-        base = 3 + 5 * kind
-        ref = fac.at[kind, theirs, c]
-        got(ref, base + 1)
-        ref2 = fac.at[kind, carried, c]
-        send(ref2, ref2, base + 3, (yp, c))
-        send(ref, ref, base + 2, mate)
+        for i in range(4):
+            shared(kind, theirs, c, 0, i)
+            share(kind, theirs, 4, i, (yp, c), b0 == 0)
+            share(kind, theirs, 2, i, mate)
 
     def factor_end(kind):
-        base = 3 + 5 * kind
-        ref = fac.at[kind, across, c]
-        got(ref, base + 3)
-        send(ref, ref, base + 4, mate)
+        for i in range(4):
+            shared(kind, across, c, 1, i)
+            share(kind, across, 3, i, mate)
 
     def factor_wait(kind, which):
-        base = 3 + 5 * kind
-        idx, slot = ((own, base), (theirs, base + 2), (across, base + 4))[which]
-        got(fac.at[kind, idx, oc], slot)
+        if which == 0:
+            got(fac.at[kind, own, oc], 3 + kind)
+        else:
+            for i in range(4):
+                shared(kind, (theirs, across)[which - 1], oc, 1 + which, i)
 
     def factor(kind, idx):
         return fac[kind, idx].reshape(width, width)
@@ -212,7 +220,7 @@
         state[pl.ds(pl.multiple_of(c * mid, mid), mid), :], couple[...]
     ).reshape(2, quarter, width)
     got(part_recv, 13)
-    xs[...] = part_own[1 - b0] + part_recv[1 - b0]
+    xs[...] = (part_own[1 - b0] + part_recv[1 - b0]).astype(BF16)
     send(xs, xr, 14, (xp, c))
     factor_x(1)
     factor_y(0)
@@ -222,10 +230,11 @@
     for h in range(2):
         arrive(r1.at[h], rrecv.at[h], jnp.logical_not(is_even & (c == h)))
     got(xr, 14)
-    taken = part_own[b0] + part_recv[b0] + xr[...]
+    taken = part_own[b0] + part_recv[b0] + xr[...].astype(F32)
     w1 = jnp.concatenate([r1[0], r1[1]], axis=1) - taken
     o1[...] = two_pass(w1, factor(0, 0), dot_nt).reshape(2, eighth, width)
-    send(o1.at[1 - b1], yr, 15, (yp, c))
+    ys[...] = o1[1 - b1].astype(BF16)
+    send(ys, yr, 15, (yp, c))
     factor_end(0)
     factor_wait(0, 2)
     last = q == planes - 1
@@ -235,13 +244,14 @@
     for h in range(2):
         arrive(rb.at[0, h], rrecv.at[2 + h], jnp.logical_not((b0 == 1) & (b1 == 0) & (c == h)))
     got(yr, 15)
-    w2 = jnp.concatenate([rb[0, 0], rb[0, 1]], axis=1) - (o1[b1] + yr[...])
+    w2 = jnp.concatenate([rb[0, 0], rb[0, 1]], axis=1) - (o1[b1] + yr[...].astype(F32))
     out2 = two_pass(w2, factor(0, 1), dot_nt)
     even_plane = q % 2 == 0
     odd_plane = jnp.logical_not(even_plane)
     zs[0] = out2
+    zb[0] = out2.astype(BF16)
     place = p % 4
-    send(zs.at[0], zr.at[1], 19, (4 * (q - 1) + place, c), odd_plane)
+    send(zb.at[0], zr.at[1], 19, (4 * (q - 1) + place, c), odd_plane)
 
     reach = 1
     for bit in range(leaves.bit_length()):
@@ -265,15 +275,17 @@
 
     @pl.when(has_node)
     def _():
-        first = jnp.where(even_plane, zs[0], zr[0])
-        w3 = jnp.concatenate([rb[1, 0], rb[1, 1]], axis=1) - (first + zr[1])
+        first = jnp.where(even_plane, zs[0], zr[0].astype(F32))
+        w3 = jnp.concatenate([rb[1, 0], rb[1, 1]], axis=1) - (first + zr[1].astype(F32))
         w3_at[...] = w3
-        zs[1] = two_pass(w3, factor(0, 2), dot_nt)
+        out3 = two_pass(w3, factor(0, 2), dot_nt)
+        zs[1] = out3
+        zb[1] = out3.astype(BF16)
 
     climbs = has_node & jnp.logical_not(joint)
     up_slot = 18 + jnp.where(upper, 1, 0)
     push(
-        zs.at[1], zr.at[jnp.where(upper, 1, 0)], send_sem.at[20], recv_sem.at[up_slot],
+        zb.at[1], zr.at[jnp.where(upper, 1, 0)], send_sem.at[20], recv_sem.at[up_slot],
         (4 * parent + place, c), climbs,
     )
 
@@ -289,25 +301,29 @@
     for which in range(3):
         factor_wait(1, which)
 
-    w3n = two_pass(w3_at[...] if False else jnp.where(has_node, w3_at[...], 0.0), factor(1, 2), dot_nn)
+    w3n = two_pass(jnp.where(has_node, w3_at[...], 0.0), factor(1, 2), dot_nn)
     got(dn.at[0], 21, climbs)
 
     @pl.when(has_node)
     def _():
-        above = jnp.where(joint, sols[0], dn[0])
-        sols[1] = w3n - two_pass(above, factor(0, 2), dot_nn)
-
-    push(sols.at[1], dn.at[0], send_sem.at[22], recv_sem.at[21], (4 * low_child + place, c), inner)
-    push(sols.at[1], dn.at[0], send_sem.at[23], recv_sem.at[21], (4 * high_child + place, c), inner)
-    push(sols.at[1], dn.at[1], send_sem.at[24], recv_sem.at[22], (4 * (q + 1) + place, c), even_plane)
+        above = jnp.where(joint, sols[0], dn[0].astype(F32))
+        sol3 = w3n - two_pass(above, factor(0, 2), dot_nn)
+        sols[1] = sol3
+        sb[...] = sol3.astype(BF16)
+
+    push(sb, dn.at[0], send_sem.at[22], recv_sem.at[21], (4 * low_child + place, c), inner)
+    push(sb, dn.at[0], send_sem.at[23], recv_sem.at[21], (4 * high_child + place, c), inner)
+    push(sb, dn.at[1], send_sem.at[24], recv_sem.at[22], (4 * (q + 1) + place, c), even_plane)
     w2n = two_pass(w2, factor(1, 1), dot_nn)
     w1n = two_pass(w1, factor(1, 0), dot_nn)
     got(dn.at[1], 22, odd_plane)
-    above2 = jnp.where(even_plane, sols[1], dn[1])
-    s1[b1] = w2n - two_pass(above2, factor(0, 1), dot_nn)
-    send(s1.at[b1], s1.at[b1], 25, (yp, c))
-    got(s1.at[1 - b1], 25)
-    sol1 = w1n - two_pass(s1[...].reshape(quarter, width), factor(0, 0), dot_nn)
+    above2 = jnp.where(even_plane, sb[...], dn[1])
+    sol2 = w2n - dot_nn(above2, factor(0, 1))
+    s1[...] = sol2
+    sh[b1] = sol2.astype(BF16)
+    send(sh.at[b1], sh.at[b1], 25, (yp, c))
+    got(sh.at[1 - b1], 25)
+    sol1 = w1n - dot_nn(sh[...].reshape(quarter, width), factor(0, 0))
     s2[...] = sol1.reshape(2, eighth, width)
     slot = c * 2 + b0
     gath[slot] = sol1.astype(BF16)
@@ -335,11 +351,11 @@
                 sep_acc[block] = s2[part_at, :, cols]
 
         here = (b0 == 1) & (b1 == 0) & (c == h)
-        push(s1.at[b1, :, cols], sep_acc.at[block8], osend.at[8 + h], orecv.at[4 + block8], (4 * q + 1, h), jnp.logical_not(here))
+        push(s1.at[:, cols], sep_acc.at[block8], osend.at[8 + h], orecv.at[4 + block8], (4 * q + 1, h), jnp.logical_not(here))
 
         @pl.when(here)
         def _():
-            sep_acc[block8] = s1[b1, :, cols]
+            sep_acc[block8] = s1[:, cols]
 
         here = (b0 == 1) & (b1 == 1) & (c == h)
         push(sols.at[1, :, cols], sep_acc.at[block8], osend.at[10 + h], orecv.at[4 + block8], (4 * q + 3, h), has_node & jnp.logical_not(here))
@@ -350,22 +366,37 @@
 
         push(sols.at[0, :, cols], sep_acc.at[block8], osend.at[12 + h], orecv.at[4 + block8], (leaves - 1, h), joint)
 
-    for t in range(1, 4):
+    def gathered(t):
         from_c = (c + t // 2) % 2
         from_b = (b0 + t % 2) % 2
         arrive(gath.at[from_c * 2 + from_b], orecv.at[t])
 
-    whole = gath[...].reshape(rows, width)
-    residue = (state[...].astype(F32) - dot_nn(whole, couple[...])).astype(BF16)
-    for j in range(4):
-        cols = pl.ds(pl.multiple_of(oc * part + j * piece, piece), piece)
-        fin_s[j] = dot_nn(residue, inv[:, cols])
-        send(fin_s.at[j], fin_r.at[j], 26 + j, mate)
-    for j in range(4):
-        cols = pl.ds(pl.multiple_of(c * part + j * piece, piece), piece)
-        value = dot_nn(residue, inv[:, cols])
-        got(fin_r.at[j], 26 + j)
-        leaf_out[:, pl.ds(j * piece, piece)] = value + fin_r[j]
+    def backward(group, side):
+        spans = [pl.ds(pl.multiple_of((2 * h + side) * quarter, quarter), quarter) for h in range(2)]
+        whole = jnp.concatenate([gath[side], gath[2 + side]], axis=0)
+        before = jnp.concatenate([state[spans[0], :], state[spans[1], :]], axis=0).astype(F32)
+        residue = (before - dot_nn(whole, couple[...])).astype(BF16)
+        for j in range(4):
+            cols = pl.ds(pl.multiple_of(oc * part + j * piece, piece), piece)
+            fin_s[group, j] = dot_nn(residue, inv[:, cols]).astype(BF16)
+            push(fin_s.at[group, j], fin_r.at[group, j], gsend.at[group, j], grecv.at[group, j], mate)
+        for j in range(4):
+            cols = pl.ds(pl.multiple_of(c * part + j * piece, piece), piece)
+            value = dot_nn(residue, inv[:, cols])
+            for h in range(2):
+                leaf_out[spans[h], pl.ds(j * piece, piece)] = value[h * quarter:(h + 1) * quarter]
+        return spans
+
+    gathered(2)
+    spans = [backward(0, b0)]
+    gathered(1)
+    gathered(3)
+    spans.append(backward(1, 1 - b0))
+    for group in range(2):
+        for j in range(4):
+            arrive(fin_r.at[group, j], grecv.at[group, j])
+            for h in range(2):
+                leaf_out[spans[group][h], pl.ds(j * piece, piece)] += fin_r[group, j, pl.ds(h * quarter, quarter)].astype(F32)
 
     for block in range(8):
         bc, bb0, bb1 = block // 4, (block // 2) % 2, block % 2
@@ -390,10 +421,7 @@
     dma = pltpu.SemaphoreType.DMA
     leaf_solution, sep_solution = pl.pallas_call(
         functools.partial(kernel, leaves),
-        out_shape=(
-            jax.ShapeDtypeStruct((rows, part), F32),
-            jax.ShapeDtypeStruct((rows, half), F32),
-        ),
+        out_shape=(pltpu.VMEM((rows, part), F32), pltpu.VMEM((rows, half), F32)),
         in_specs=[vmem, anywhere, anywhere, vmem, vmem, vmem],
         out_specs=(vmem, vmem),
         scratch_shapes=[
@@ -401,11 +429,13 @@
             V((half, width), F32), V((half, half), F32), V((2, 3, 2, half, width), BF16), V((2, half, width), BF16),
             V((2, quarter, half), F32), V((2, 2, eighth, half), F32), V((2, eighth, half), F32),
             V((2, quarter, width), F32), V((2, quarter, width), F32), V((2, quarter, width), F32),
-            V((quarter, width), F32), V((quarter, width), F32), V((2, eighth, width), F32), V((eighth, width), F32),
-            V((2, eighth, width), F32), V((2, eighth, width), F32), V((2, eighth, width), F32), V((2, eighth, width), F32),
-            V((2, eighth, width), F32), V((2, eighth, width), F32), V((4, quarter, width), BF16),
-            V((4, rows, part // 4), F32), V((4, rows, part // 4), F32), V((8, eighth, half), F32),
-            dma((2,)), dma((30,)), dma((30,)), dma((20,)), dma((8,)), dma((14,)), dma((12,)),
+            V((quarter, width), BF16), V((quarter, width), BF16), V((2, eighth, width), F32), V((eighth, width), BF16),
+            V((eighth, width), BF16), V((2, eighth, width), F32), V((2, eighth, width), BF16), V((2, eighth, width), BF16),
+            V((2, eighth, width), F32), V((eighth, width), BF16), V((2, eighth, width), BF16), V((2, eighth, width), F32),
+            V((eighth, width), F32), V((2, eighth, width), BF16), V((4, quarter, width), BF16),
+            V((2, 4, rows // 2, part // 4), BF16), V((2, 4, rows // 2, part // 4), BF16), V((8, eighth, half), F32),
+            dma((2,)), dma((30,)), dma((30,)), dma((2, 5, 4)), dma((2, 5, 4)), dma((20,)), dma((8,)), dma((14,)), dma((12,)),
+            dma((2, 4)), dma((2, 4)),
         ],
         compiler_params=pltpu.CompilerParams(
             collective_id=0, has_side_effects=True, vmem_limit_bytes=60 * 1024 * 1024

time: 64.8 us -> 52.8 us (0.81); the launches traced: 63.6 us -> 52.7 us
  Pallas kernels: 59 us -> 50.4 us
  local copies, waits for them, and re-layouts: 3.98 us -> 1.67 us
    pallas_call x1, Pallas kernels: 59 us -> 50.4 us  [local(): pl.pallas_call(functools.partial(kernel, leaves), out_shape=(pltpu.VMEM((...]
    unnamed x2, local copies, waits for them, and re-layouts: 3.98 us -> 1.67 us
where the time goes in v2:
time: 52.8 us; the launch traced here: 52.7 us
  Pallas kernels  50.4 us (95%)
  local copies, waits for them, and re-layouts  1.67 us (3%)
  between operations  0.64 us (1%)
    pallas_call x1, Pallas kernels, local(): pl.pallas_call(functools.partial(kernel, leaves), out_shape=(pltpu.VMEM((...  50.4 us
    unnamed x2, local copies, waits for them, and re-layouts  1.67 us

profile of v2, /device:TPU:11, one launch (start us, length us, event | category | flops | bytes accessed | tf_op | source)
XLA Modules:
  0.0 52.7 jit_solution(14941375765766003810)
XLA Ops:
  0.6 50.4 %shard_map.77 = (f32[256,1024]{1,0:T(8,128)S(1)}, f32[256,256]{1,0:T(8,128)S(1)}) custom-call(bf16[256,1024]{1,0:T(8,128)(2,1)} %bitcast.8, bf16[1,1024,2048]{2,1,0:T(8,128)(2,1)} %inv_hbm.1, bf16[1,512,1024]{2,1,0:T(8,128)(2,1)} %couple_hbm.1, f32[256,256]{1,0:T(8,128)} %bitcast.11, f32[256,512]{1,0:T(8,128)} %bitcast.9, f32[512,256]{1,0:T(8,128)} %bitcast.10), custom_call_target="tpu_custom_call" | custom-call | tf_op jit(solution)/shard_map/pallas_call | solution.py:422
  51.0 1.0 %copy.10 = f32[1,256,1024]{2,1,0:T(8,128)} copy(f32[1,256,1024]{2,1,0:T(8,128)S(1)} %bitcast.6) | data formatting | bytes 2097152
  52.0 0.7 %copy.11 = f32[1,256,256]{2,1,0:T(8,128)} copy(f32[1,256,256]{2,1,0:T(8,128)S(1)} %bitcast.7) | data formatting | bytes 524288

commit v3 on v2

--- a/solution.py
+++ b/solution.py
@@ -47,7 +47,7 @@
     inv, couple, other_rhs, state, other_inv, other_cpl, fac, top,
     r1, rb, rt, part_send, part_own, part_recv, xs, xr, o1, yr,
     ys, zs, zb, zr, sols, sb, dn, s2, s1, sh, gath, fin_s, fin_r, sep_acc,
-    load_sem, send_sem, recv_sem, fsend, frecv, rsend, rrecv, osend, orecv, gsend, grecv,
+    load_sem, send_sem, recv_sem, fsend, frecv, rsend, rrecv, osend, orecv, gsend, grecv, tsend, trecv,
 ):
     p = lax.axis_index("leaf")
     c = lax.axis_index("sep")
@@ -155,26 +155,48 @@
     got(other_cpl, 2)
     at = pl.ds(pl.multiple_of(c * half, half), half)
     ours = scpl_ref[at, :]
-    m_rows = three_pass(ours, sinv_ref[...], dot_nn) + three_pass(other_cpl[...], other_inv[...], dot_nn)
-    n_rows = three_pass(sinv_ref[:, at], sinv_ref[...], dot_tn) + three_pass(other_inv[:, at], other_inv[...], dot_tn)
-    fac[0, own, c] = jnp.where(is_top, n_rows, m_rows).astype(BF16)
-    fac[1, own, c] = n_rows.astype(BF16)
+
+    def n_rows():
+        mine, other = sinv_ref[:, at], other_inv[:, at]
+        return (three_pass(mine, sinv_ref[...], dot_tn) + three_pass(other, other_inv[...], dot_tn)).astype(BF16)
+
+    @pl.when(is_top)
+    def _():
+        fac[0, own, c] = n_rows()
+
+    @pl.when(jnp.logical_not(is_top))
+    def _():
+        m_rows = three_pass(ours, sinv_ref[...], dot_nn) + three_pass(other_cpl[...], other_inv[...], dot_nn)
+        fac[0, own, c] = m_rows.astype(BF16)
+
     theirs = (1 - b0) * (1 + b1)
     across = 2 - b1
 
     chunk = half // 4
+    last = q == planes - 1
+    joint = q == below_top
+    place = p % 4
+
+    def top_share(i, cond):
+        span = pl.ds(i * chunk, chunk)
+        push(
+            fac.at[0, 2, c, span], top.at[c, span], tsend.at[i], trecv.at[i],
+            (4 * below_top + place, c), last & cond,
+        )
 
     def share(kind, idx, path, i, to, cond=None):
         ref = fac.at[kind, idx, c, pl.ds(i * chunk, chunk)]
         push(ref, ref, fsend.at[kind, path, i], frecv.at[kind, 1 if path == 4 else path, i], to, cond)
 
-    def shared(kind, idx, core, path, i):
-        arrive(fac.at[kind, idx, core, pl.ds(i * chunk, chunk)], frecv.at[kind, path, i])
+    def shared(kind, idx, core, path, i, cond=None):
+        arrive(fac.at[kind, idx, core, pl.ds(i * chunk, chunk)], frecv.at[kind, path, i], cond)
 
     def factor_x(kind):
         for i in range(4):
             share(kind, own, 0, i, (xp, c))
-            share(kind, own, 1, i, (yp, c), b0 == 1)
+            if kind == 0:
+                share(kind, own, 1, i, (yp, c), b0 == 1)
+                top_share(i, (b0 == 1) & (b1 == 1))
         ref = fac.at[kind, own, c]
         send(ref, ref, 3 + kind, mate)
 
@@ -183,11 +205,13 @@
             shared(kind, theirs, c, 0, i)
             share(kind, theirs, 4, i, (yp, c), b0 == 0)
             share(kind, theirs, 2, i, mate)
-
-    def factor_end(kind):
+            if kind == 0:
+                top_share(i, (b0 == 0) & (b1 == 1))
+
+    def factor_end(kind, cond=None):
         for i in range(4):
-            shared(kind, across, c, 1, i)
-            share(kind, across, 3, i, mate)
+            shared(kind, across, c, 1, i, cond)
+            share(kind, across, 3, i, mate, cond)
 
     def factor_wait(kind, which):
         if which == 0:
@@ -200,6 +224,7 @@
         return fac[kind, idx].reshape(width, width)
 
     factor_x(0)
+    fac[1, own, c] = n_rows()
 
     got(other_rhs, 0)
     loads[1].wait()
@@ -224,6 +249,9 @@
     send(xs, xr, 14, (xp, c))
     factor_x(1)
     factor_y(0)
+    factor_end(0, b0 == 1)
+    for i in range(4):
+        top_share(i, (b0 == 1) & (b1 == 0))
     factor_wait(0, 0)
     factor_wait(0, 1)
 
@@ -235,11 +263,10 @@
     o1[...] = two_pass(w1, factor(0, 0), dot_nt).reshape(2, eighth, width)
     ys[...] = o1[1 - b1].astype(BF16)
     send(ys, yr, 15, (yp, c))
-    factor_end(0)
+    for i in range(4):
+        share(1, own, 1, i, (yp, c), b0 == 1)
+    factor_end(0, b0 == 0)
     factor_wait(0, 2)
-    last = q == planes - 1
-    joint = q == below_top
-    send(fac.at[0, 2, c], top.at[c], 16, (4 * below_top + p % 4, c), last)
 
     for h in range(2):
         arrive(rb.at[0, h], rrecv.at[2 + h], jnp.logical_not((b0 == 1) & (b1 == 0) & (c == h)))
@@ -250,8 +277,9 @@
     odd_plane = jnp.logical_not(even_plane)
     zs[0] = out2
     zb[0] = out2.astype(BF16)
-    place = p % 4
     send(zb.at[0], zr.at[1], 19, (4 * (q - 1) + place, c), odd_plane)
+    for i in range(4):
+        top_share(i, (b0 == 0) & (b1 == 0))
 
     reach = 1
     for bit in range(leaves.bit_length()):
@@ -264,7 +292,8 @@
     inner = odd_plane & has_node
 
     factor_y(1)
-    got(top.at[c], 16, joint)
+    for i in range(4):
+        arrive(top.at[c, pl.ds(i * chunk, chunk)], trecv.at[i], joint)
     send(top.at[c], top.at[c], 17, mate, joint)
 
     for h in range(2):
@@ -435,7 +464,7 @@
             V((eighth, width), F32), V((2, eighth, width), BF16), V((4, quarter, width), BF16),
             V((2, 4, rows // 2, part // 4), BF16), V((2, 4, rows // 2, part // 4), BF16), V((8, eighth, half), F32),
             dma((2,)), dma((30,)), dma((30,)), dma((2, 5, 4)), dma((2, 5, 4)), dma((20,)), dma((8,)), dma((14,)), dma((12,)),
-            dma((2, 4)), dma((2, 4)),
+            dma((2, 4)), dma((2, 4)), dma((4,)), dma((4,)),
         ],
         compiler_params=pltpu.CompilerParams(
             collective_id=0, has_side_effects=True, vmem_limit_bytes=60 * 1024 * 1024

time: 52.8 us -> 51.3 us (0.972)
  Pallas kernels: 50.4 us -> 48.8 us
    pallas_call x1, Pallas kernels: 50.4 us -> 48.8 us  [local(): pl.pallas_call(functools.partial(kernel, leaves), out_shape=(pltpu.VMEM((...]
where the time goes in v3:
time: 51.3 us; the launch traced here: 51.1 us
  Pallas kernels  48.8 us (95%)
  local copies, waits for them, and re-layouts  1.67 us (3%)
  between operations  0.64 us (1%)
    pallas_call x1, Pallas kernels, local(): pl.pallas_call(functools.partial(kernel, leaves), out_shape=(pltpu.VMEM((...  48.8 us
    unnamed x2, local copies, waits for them, and re-layouts  1.67 us

profile of v3, /device:TPU:11, one launch (start us, length us, event | category | flops | bytes accessed | tf_op | source)
XLA Modules:
  0.0 51.1 jit_solution(6534874592717111331)
XLA Ops:
  0.6 48.8 %shard_map.77 = (f32[256,1024]{1,0:T(8,128)S(1)}, f32[256,256]{1,0:T(8,128)S(1)}) custom-call(bf16[256,1024]{1,0:T(8,128)(2,1)} %bitcast.8, bf16[1,1024,2048]{2,1,0:T(8,128)(2,1)} %inv_hbm.1, bf16[1,512,1024]{2,1,0:T(8,128)(2,1)} %couple_hbm.1, f32[256,256]{1,0:T(8,128)} %bitcast.11, f32[256,512]{1,0:T(8,128)} %bitcast.9, f32[512,256]{1,0:T(8,128)} %bitcast.10), custom_call_target="tpu_custom_call" | custom-call | tf_op jit(solution)/shard_map/pallas_call | solution.py:451
  49.4 1.0 %copy.10 = f32[1,256,1024]{2,1,0:T(8,128)} copy(f32[1,256,1024]{2,1,0:T(8,128)S(1)} %bitcast.6) | data formatting | bytes 2097152
  50.4 0.7 %copy.11 = f32[1,256,256]{2,1,0:T(8,128)} copy(f32[1,256,256]{2,1,0:T(8,128)S(1)} %bitcast.7) | data formatting | bytes 524288
